TPU v7x, 32 devices: a whole 2x2x4 slice. The times are simulated.
32 devices in a mesh: dp: 2 (over core), wide: 4 (over y, x), narrow: 4 (over z).
Axes of the slice: x: 2, y: 2, z: 4, core: 2. Of those that a mesh axis runs over, the one named last changes fastest.
Arguments:
- block_input: float32 [1600, 4096], P('wide', ('dp', 'narrow')), as said below
- block_cotangent: float32 [1600, 4096], P('wide', ('dp', 'narrow')), may hold values from -6 to 6
- seq_start: int32 [32, 128], P(('dp', 'wide', 'narrow')), may hold values from 0 to 127, as said below
- ln1_gain: float32 [1600], P('wide'), may hold values from 0.5 to 1.5
- ln1_shift: float32 [1600], P('wide'), may hold values from -2 to 2
- w_qkv: float32 [1600, 3, 1600], P('wide', None, 'narrow'), may hold values from -0.15625 to 0.15625
- b_qv: float32 [2, 1600], P(None, 'narrow'), may hold values from -3 to 3
- w_out: float32 [1600, 1600], P('wide', 'narrow'), may hold values from -0.4375 to 0.4375
- b_out: float32 [1600], P('wide'), may hold values from -2 to 2
- ln2_gain: float32 [1600], P('wide'), may hold values from 0.5 to 1.5
- ln2_shift: float32 [1600], P('wide'), may hold values from -2 to 2
- w_fc: float32 [1600, 6400], P('wide', 'narrow'), may hold values from -0.15625 to 0.15625
- b_fc: float32 [6400], P('narrow'), may hold values from -3 to 3
- w_proj: float32 [1600, 6400], P('wide', 'narrow'), may hold values from -0.078125 to 0.078125
- b_proj: float32 [1600], P('wide'), may hold values from -2 to 2
Outputs:
- block_output: float32 [1600, 4096], P('wide', ('dp', 'narrow'))
- input_grad: float32 [1600, 4096], P('wide', ('dp', 'narrow'))
- grad_ln1_gain: float32 [1600], P('wide')
- grad_ln1_shift: float32 [1600], P('wide')
- grad_w_qkv: float32 [1600, 3, 1600], P('wide', None, 'narrow')
- grad_b_qv: float32 [2, 1600], P(None, 'narrow')
- grad_w_out: float32 [1600, 1600], P('wide', 'narrow')
- grad_b_out: float32 [1600], P('wide')
- grad_ln2_gain: float32 [1600], P('wide')
- grad_ln2_shift: float32 [1600], P('wide')
- grad_w_fc: float32 [1600, 6400], P('wide', 'narrow')
- grad_b_fc: float32 [6400], P('narrow')
- grad_w_proj: float32 [1600, 6400], P('wide', 'narrow')
- grad_b_proj: float32 [1600], P('wide')
Inputs may be any that keep to these rules, and one draw needn't show every extreme that they name: `block_input`: token activations of order one, with scales that differ from token to token. `seq_start`: along each row the values never fall; each equals the token's own position at the first token of its sequence and the start of its sequence after it. Block 0 holds one sequence of 128 tokens; some block ends with a sequence of one token.
All inputs are finite; a program needn't handle non-finite values.
Results may differ from a plain program's by a relative error of at most 0.011.
Values may be sent and summed in bfloat16 or wider, within the bound.
A program may use at most 320 MiB of HBM per device.

v0:
```python
import math
import jax
import jax.numpy as jnp
from jax import lax
from jax.sharding import PartitionSpec as P

HEADS = 25
HEAD = 64
EPS = 1e-05
GELU_C = math.sqrt(2.0 / math.pi)


def gelu_value(pre_act):
    inner = GELU_C * (pre_act + 0.044715 * pre_act * pre_act * pre_act)
    return 0.5 * pre_act * (1.0 + jnp.tanh(inner))


def gelu_slope(pre_act):
    tanh_part = jnp.tanh(GELU_C * (pre_act + 0.044715 * pre_act * pre_act * pre_act))
    return 0.5 * (1.0 + tanh_part) + 0.5 * pre_act * (1.0 - tanh_part * tanh_part) * GELU_C * (
        1.0 + 3.0 * 0.044715 * pre_act * pre_act
    )


def row_totals(first_term, second_term):
    return lax.psum(
        (jnp.sum(first_term, axis=1, keepdims=True), jnp.sum(second_term, axis=1, keepdims=True)),
        "wide",
    )


def norm_forward(inputs, gain_shard, shift_shard):
    full_width = inputs.shape[1] * lax.axis_size("wide")
    total_sum, square_sum = row_totals(inputs, inputs * inputs)
    mean_row = total_sum / full_width
    inv_std = lax.rsqrt(square_sum / full_width - mean_row * mean_row + EPS)
    normed = (inputs - mean_row) * inv_std
    return (normed, inv_std, (normed * gain_shard + shift_shard).astype(jnp.bfloat16))


def norm_backward(row_grads, normed, inv_std, gain_shard):
    full_width = row_grads.shape[1] * lax.axis_size("wide")
    scaled = row_grads * gain_shard
    first_sum, second_sum = row_totals(scaled, scaled * normed)
    return inv_std * (scaled - first_sum / full_width - normed * (second_sum / full_width))


def gather_narrow(values):
    return lax.all_gather(values, "narrow", axis=0, tiled=True)


def sum_narrow(partial_value):
    return lax.psum_scatter(partial_value, "narrow", scatter_dimension=0, tiled=True)


def sum_wide(gathered, weight_bf, transposed):

    def partial_rows():
        if transposed:
            return lax.dot_general(
                gathered, weight_bf, (((1,), (1,)), ((), ())), preferred_element_type=jnp.float32
            )
        return jnp.dot(gathered, weight_bf, preferred_element_type=jnp.float32)

    return lax.psum_scatter(partial_rows(), "wide", scatter_dimension=0, tiled=True)


def project_wide(activations, weight_bf):
    return sum_narrow(
        jnp.dot(
            lax.all_gather(activations, "wide", axis=0, tiled=True),
            weight_bf,
            preferred_element_type=jnp.float32,
        )
    )


def fold_wide(grad_rows, inputs_all, weight_bf):
    block_rows = lax.all_gather(grad_rows, "wide", axis=0, tiled=True)
    weight_grad = lax.dot_general(
        inputs_all, block_rows, (((0,), (0,)), ((), ())), preferred_element_type=jnp.float32
    )
    back_rows = lax.dot_general(
        block_rows, weight_bf, (((1,), (1,)), ((), ())), preferred_element_type=jnp.float32
    )
    weight_grad, partial_value = (weight_grad, back_rows)
    return (weight_grad, sum_narrow(partial_value))


def weight_grad_block(activations, grads_all):
    return lax.dot_general(
        lax.all_gather(activations, "wide", axis=0, tiled=True),
        grads_all,
        (((0,), (0,)), ((), ())),
        preferred_element_type=jnp.float32,
    )


def to_heads(values):
    return lax.all_to_all(values, "narrow", split_axis=0, concat_axis=2, tiled=True)


def from_heads(values):
    return lax.all_to_all(values, "narrow", split_axis=2, concat_axis=0, tiled=True)


def block_mask(starts):
    position = jnp.arange(starts.shape[0])
    return (position[None, :] <= position[:, None]) & (starts[:, None] == starts[None, :])


def split_heads(values):
    return values.reshape(values.shape[0], HEADS, HEAD)


def attend_forward(heads_all, allowed):
    score_scale = 1.0 / math.sqrt(HEAD)
    queries = split_heads(heads_all[:, 0])
    keys_part = split_heads(heads_all[:, 1])
    values_part = split_heads(heads_all[:, 2])
    scores = (
        jnp.einsum("ihd,jhd->hij", queries, keys_part, preferred_element_type=jnp.float32)
        * score_scale
    )
    log_total = jnp.log(jnp.sum(jnp.where(allowed, jnp.exp(scores), 0.0), axis=2, keepdims=True))
    attn_probs = jnp.where(allowed, jnp.exp(scores - log_total), 0.0).astype(jnp.bfloat16)
    attended = jnp.einsum(
        "hij,jhd->ihd", attn_probs, values_part, preferred_element_type=jnp.float32
    )
    return (attended.reshape(heads_all.shape[0], HEADS * HEAD).astype(jnp.bfloat16), log_total)


def attend_backward(heads_all, allowed, log_total, attended_cot):
    score_scale = 1.0 / math.sqrt(HEAD)
    queries = split_heads(heads_all[:, 0])
    keys_part = split_heads(heads_all[:, 1])
    values_part = split_heads(heads_all[:, 2])
    scores = (
        jnp.einsum("ihd,jhd->hij", queries, keys_part, preferred_element_type=jnp.float32)
        * score_scale
    )
    probs_full = jnp.where(allowed, jnp.exp(scores - log_total), 0.0)
    cot_heads = split_heads(attended_cot)
    dprobs = jnp.einsum("ihd,jhd->hij", cot_heads, values_part, preferred_element_type=jnp.float32)
    row_delta = jnp.sum(probs_full * dprobs, axis=2, keepdims=True)
    score_cot = (probs_full * (dprobs - row_delta) * score_scale).astype(jnp.bfloat16)
    query_grad = jnp.einsum(
        "hij,jhd->ihd", score_cot, keys_part, preferred_element_type=jnp.float32
    )
    key_grad = jnp.einsum("hij,ihd->jhd", score_cot, queries, preferred_element_type=jnp.float32)
    value_grad = jnp.einsum(
        "hij,ihd->jhd",
        probs_full.astype(jnp.bfloat16),
        cot_heads,
        preferred_element_type=jnp.float32,
    )
    stacked = jnp.stack([query_grad, key_grad, value_grad], axis=1)
    return stacked.reshape(heads_all.shape[0], 3, HEADS * HEAD)


def local(
    block_input,
    block_cotangent,
    seq_start,
    ln1_gain,
    ln1_shift,
    w_qkv,
    b_qv,
    w_out,
    b_out,
    ln2_gain,
    ln2_shift,
    w_fc,
    b_fc,
    w_proj,
    b_proj,
):
    narrow_count = lax.axis_size("narrow")
    narrow_index = lax.axis_index("narrow")
    part_width = w_qkv.shape[2]
    hidden_width = w_fc.shape[1]
    rows_input = block_input.T
    rows_cot = block_cotangent.T
    wq_bf = w_qkv.astype(jnp.bfloat16).reshape(w_qkv.shape[0], 3 * part_width)
    wo_bf = w_out.T.astype(jnp.bfloat16)
    wf_bf = w_fc.astype(jnp.bfloat16)
    wp_bf = w_proj.T.astype(jnp.bfloat16)
    bias_three = jnp.stack([b_qv[0], jnp.zeros_like(b_qv[0]), b_qv[1]])
    normed_one, inv_one, norm_one = norm_forward(rows_input, ln1_gain, ln1_shift)
    norm_one_all = gather_narrow(norm_one)
    qkv_rows = sum_wide(norm_one_all, wq_bf, False)
    grid_rows = qkv_rows.shape[0]
    qkv_grid = (qkv_rows.reshape(grid_rows, 3, part_width) + bias_three).astype(jnp.bfloat16)
    heads_all = to_heads(qkv_grid)
    block_rows = heads_all.shape[0]
    allowed = block_mask(seq_start[0])
    attended, log_total = attend_forward(heads_all, allowed)
    attended_grid = from_heads(attended.reshape(block_rows, 1, HEADS * HEAD)).reshape(
        grid_rows, part_width
    )
    residual = rows_input + project_wide(attended_grid, wo_bf) + b_out
    normed_two, inv_two, norm_two = norm_forward(residual, ln2_gain, ln2_shift)
    norm_two_all = gather_narrow(norm_two)
    pre_act = sum_wide(norm_two_all, wf_bf, False) + b_fc
    hidden = gelu_value(pre_act).astype(jnp.bfloat16)
    output_rows = residual + project_wide(hidden, wp_bf) + b_proj
    cot_rows = rows_cot.astype(jnp.bfloat16)
    cot_all = gather_narrow(cot_rows)
    grad_w_proj = weight_grad_block(hidden, cot_all)
    pre_grad = sum_wide(cot_all, wp_bf, True) * gelu_slope(pre_act)
    pre_cot = pre_grad.astype(jnp.bfloat16)
    grad_w_fc, norm_two_grad = fold_wide(pre_cot, norm_two_all, wf_bf)
    resid_grad = rows_cot + norm_backward(norm_two_grad, normed_two, inv_two, ln2_gain)
    resid_cot = resid_grad.astype(jnp.bfloat16)
    resid_all = gather_narrow(resid_cot)
    grad_w_out = weight_grad_block(attended_grid, resid_all)
    attended_cot = sum_wide(resid_all, wo_bf, True).astype(jnp.bfloat16)
    cot_heads = to_heads(attended_cot.reshape(grid_rows, 1, part_width)).reshape(
        block_rows, HEADS * HEAD
    )
    qkv_grad = attend_backward(heads_all, allowed, log_total, cot_heads)
    qkv_cot = from_heads(qkv_grad.astype(jnp.bfloat16))
    grad_w_qkv, norm_one_grad = fold_wide(
        qkv_cot.reshape(grid_rows, 3 * part_width), norm_one_all, wq_bf
    )
    grad_input_rows = resid_grad + norm_backward(norm_one_grad, normed_one, inv_one, ln1_gain)
    qkv_sums = jnp.sum(qkv_grad, axis=0)
    bias_qv_full = jnp.stack([qkv_sums[0], qkv_sums[2]])
    fc_full = jnp.zeros((narrow_count * hidden_width,), jnp.float32)
    fc_full = lax.dynamic_update_slice_in_dim(
        fc_full, jnp.sum(pre_grad, axis=0), narrow_index * hidden_width, 0
    )
    bias_qv_sum, fc_sum = lax.psum((bias_qv_full, fc_full), ("dp", "wide", "narrow"))
    grad_b_qv = lax.dynamic_slice_in_dim(bias_qv_sum, narrow_index * part_width, part_width, 1)
    grad_b_fc = lax.dynamic_slice_in_dim(fc_sum, narrow_index * hidden_width, hidden_width, 0)
    row_terms = (
        jnp.sum(norm_one_grad * normed_one, axis=0),
        jnp.sum(norm_one_grad, axis=0),
        jnp.sum(resid_grad, axis=0),
        jnp.sum(norm_two_grad * normed_two, axis=0),
        jnp.sum(norm_two_grad, axis=0),
        jnp.sum(rows_cot, axis=0),
    )
    gain_one_grad, shift_one_grad, out_bias_grad, gain_two_grad, shift_two_grad, proj_bias_grad = (
        lax.psum(
            (row_terms[0], row_terms[1], row_terms[2], row_terms[3], row_terms[4], row_terms[5]),
            ("dp", "narrow"),
        )
    )
    qkv_total, out_total, fc_total, proj_total = lax.psum(
        (grad_w_qkv.reshape(w_qkv.shape), grad_w_out.T, grad_w_fc, grad_w_proj.T), "dp"
    )
    return (
        output_rows.T,
        grad_input_rows.T,
        gain_one_grad,
        shift_one_grad,
        qkv_total,
        grad_b_qv,
        out_total,
        out_bias_grad,
        gain_two_grad,
        shift_two_grad,
        fc_total,
        grad_b_fc,
        proj_total,
        proj_bias_grad,
    )


def solution(mesh):
    return jax.shard_map(
        local,
        mesh=mesh,
        in_specs=(
            P("wide", ("dp", "narrow")),
            P("wide", ("dp", "narrow")),
            P(("dp", "wide", "narrow"), None),
            P("wide"),
            P("wide"),
            P("wide", None, "narrow"),
            P(None, "narrow"),
            P("wide", "narrow"),
            P("wide"),
            P("wide"),
            P("wide"),
            P("wide", "narrow"),
            P("narrow"),
            P("wide", "narrow"),
            P("wide"),
        ),
        out_specs=(
            P("wide", ("dp", "narrow")),
            P("wide", ("dp", "narrow")),
            P("wide"),
            P("wide"),
            P("wide", None, "narrow"),
            P(None, "narrow"),
            P("wide", "narrow"),
            P("wide"),
            P("wide"),
            P("wide"),
            P("wide", "narrow"),
            P("narrow"),
            P("wide", "narrow"),
            P("wide"),
        ),
        check_vma=False,
    )
```

profile of v0, /device:TPU:0, one launch (start us, length us, event | category | flops | bytes accessed | tf_op | source)
XLA Modules:
  0.0 1337.4 jit_solution(5024976810314251157)
XLA Ops:
  7.3 1.3 fusion.27
  9.8 11.4 all-reduce.5
  22.2 1.9 convert_element_type.65
  25.0 34.8 %all-gather.9.cloned.1.call-done = bf16[2048,400]{0,1:T(8,128)(2,1)} async-done(((bf16[512,400]{0,1:T(8,128)(2,1)}), bf16[2048,400]{0,1:T(8,128)(2,1)}) %all-gather.9.cloned.1.call-update) | async-done | bytes 1638416 | tf_op jit(solution)/shard_map/all_gather | solution.py:49
  59.8 6.7 fusion.89
  67.2 96.4 %reduce-scatter.9.cloned.1.call-done = f32[512,1200]{0,1:T(8,128)} async-done(((f32[2048,1200]{0,1:T(8,128)}), f32[512,1200]{0,1:T(8,128)}) %reduce-scatter.9.cloned.1.call-update) | async-done | bytes 2457616 | tf_op jit(solution)/shard_map/reduce_scatter | solution.py:65
  163.6 1.9 add_convert_fusion
  165.5 3.0 copy.135
  168.5 4.7 all-to-all-start
  173.5 47.8 %all-to-all-done = bf16[512,3,400]{2,1,0:T(4,128)(2,1)S(1)} async-done(((bf16[512,3,400]{2,1,0:T(4,128)(2,1)}), bf16[512,3,400]{2,1,0:T(4,128)(2,1)S(1)}, u32[]{:S(2)}, u32[]{:S(2)}) %all-to-all-start) | async-done | bytes 1228832 | tf_op jit(solution)/shard_map/all_to_all | solution.py:100
  221.2 2.5 copy.136
  223.7 1.3 fusion.79
  227.4 6.3 copy.168
  234.3 9.1 reduce.2
  243.5 14.0 %all_to_all.63 = bf16[4,2,25600]{2,1,0:T(2,128)(2,1)S(1)} all-to-all(bf16[4,2,25600]{2,1,0:T(2,128)(2,1)S(1)} %reshape.90), channel_id=1, replica_groups=mesh['dp'=2,'wide'=4,'narrow'=4] {'narrow'}, dimensions={0} | all-to-all | bytes 819200 | tf_op jit(solution)/shard_map/all_to_all | solution.py:104
  259.0 29.5 %all-gather.11.cloned.1.call-done = bf16[2048,400]{0,1:T(8,128)(2,1)} async-done(((bf16[512,400]{0,1:T(8,128)(2,1)}), bf16[2048,400]{0,1:T(8,128)(2,1)}) %all-gather.11.cloned.1.call-update) | async-done | bytes 1638416 | tf_op jit(solution)/shard_map/all_gather | solution.py:71
  288.5 4.1 fusion.55
  294.6 60.6 %reduce-scatter.11.cloned.1.call-done = f32[512,400]{0,1:T(8,128)} async-done(((f32[2048,400]{0,1:T(8,128)}), f32[512,400]{0,1:T(8,128)}) %reduce-scatter.11.cloned.1.call-update) | async-done | bytes 819216 | tf_op jit(solution)/shard_map/reduce_scatter | solution.py:53
  355.2 1.3 fusion.74
  356.6 9.8 all-reduce.4
  367.7 27.7 %all-gather.17.cloned.1.call-done = bf16[2048,400]{0,1:T(8,128)(2,1)} async-done(((bf16[512,400]{0,1:T(8,128)(2,1)}), bf16[2048,400]{0,1:T(8,128)(2,1)}) %all-gather.17.cloned.1.call-update) | async-done | bytes 1638416 | tf_op jit(solution)/shard_map/all_gather | solution.py:49
  395.4 10.6 fusion.34
  406.1 28.3 %all-gather.13.cloned.1.call-done = bf16[2048,400]{0,1:T(8,128)(2,1)} async-done(((bf16[512,400]{0,1:T(8,128)(2,1)}), bf16[2048,400]{0,1:T(8,128)(2,1)}) %all-gather.13.cloned.1.call-update) | async-done | bytes 1638416 | tf_op jit(solution)/shard_map/all_gather | solution.py:49
  434.3 11.3 fusion.40
  445.7 115.5 %reduce-scatter.17.cloned.1.call-done = f32[512,1600]{0,1:T(8,128)} async-done(((f32[2048,1600]{0,1:T(8,128)}), f32[512,1600]{0,1:T(8,128)}) %reduce-scatter.17.cloned.1.call-update) | async-done | bytes 3276816 | tf_op jit(solution)/shard_map/reduce_scatter | solution.py:65
  561.2 128.0 %reduce-scatter.13.cloned.1.call-done = f32[512,1600]{0,1:T(8,128)} async-done(((f32[2048,1600]{0,1:T(8,128)}), f32[512,1600]{0,1:T(8,128)}) %reduce-scatter.13.cloned.1.call-update) | async-done | bytes 3276816 | tf_op jit(solution)/shard_map/reduce_scatter | solution.py:65
  689.3 5.9 fusion.75
  695.8 71.6 %all-gather.19.cloned.1.call-done = bf16[2048,1600]{0,1:T(8,128)(2,1)} async-done(((bf16[512,1600]{0,1:T(8,128)(2,1)}), bf16[2048,1600]{0,1:T(8,128)(2,1)}) %all-gather.19.cloned.1.call-update) | async-done | bytes 6553616 | tf_op jit(solution)/shard_map/all_gather | solution.py:79
  767.4 8.5 fusion.38
  776.4 65.4 %all-gather.15.cloned.1.call-done = bf16[2048,1600]{0,1:T(8,128)(2,1)} async-done(((bf16[512,1600]{0,1:T(8,128)(2,1)}), bf16[2048,1600]{0,1:T(8,128)(2,1)}) %all-gather.15.cloned.1.call-update) | async-done | bytes 6553616 | tf_op jit(solution)/shard_map/all_gather | solution.py:71
  841.8 8.5 fusion.36
  850.3 56.2 %reduce-scatter.19.cloned.1.call-done = f32[512,400]{0,1:T(8,128)} async-done(((f32[2048,400]{0,1:T(8,128)}), f32[512,400]{0,1:T(8,128)}) %reduce-scatter.19.cloned.1.call-update) | async-done | bytes 819216 | tf_op jit(solution)/shard_map/reduce_scatter | solution.py:53
  906.6 1.5 multiply_reduce_fusion.1
  908.1 9.9 all-reduce.3
  917.9 53.2 %reduce-scatter.15.cloned.1.call-done = f32[512,400]{0,1:T(8,128)} async-done(((f32[2048,400]{0,1:T(8,128)}), f32[512,400]{0,1:T(8,128)}) %reduce-scatter.15.cloned.1.call-update) | async-done | bytes 819216 | tf_op jit(solution)/shard_map/reduce_scatter | solution.py:53
  971.2 3.5 fusion.77
  975.5 38.2 %all-gather.21.cloned.1.call-done = bf16[2048,400]{0,1:T(8,128)(2,1)} async-done(((bf16[512,400]{0,1:T(8,128)(2,1)}), bf16[2048,400]{0,1:T(8,128)(2,1)}) %all-gather.21.cloned.1.call-update) | async-done | bytes 1638416 | tf_op jit(solution)/shard_map/all_gather | solution.py:49
  1013.7 4.2 fusion.53
  1017.9 44.0 %reduce-scatter.21.cloned.1.call-done = f32[512,400]{0,1:T(8,128)} async-done(((f32[2048,400]{0,1:T(8,128)}), f32[512,400]{0,1:T(8,128)}) %reduce-scatter.21.cloned.1.call-update) | async-done | bytes 819216 | tf_op jit(solution)/shard_map/reduce_scatter | solution.py:65
  1063.1 1.7 reduce.3
  1066.0 1.7 reshape.92
  1067.7 4.6 all-to-all-start.2
  1072.4 2.1 fusion.11
  1074.5 9.7 all-to-all-done.2
  1087.2 1.6 fusion.84
  1088.8 3.5 fusion.22
  1092.2 3.9 fusion.19
  1096.1 3.7 fusion.42
  1099.8 3.4 fusion.9
  1103.1 40.4 %all_to_all.64 = bf16[128,3,1600]{0,1,2:T(4,128)(2,1)S(1)} all-to-all(bf16[128,3,1600]{0,1,2:T(4,128)(2,1)S(1)} %fusion.9), channel_id=1, replica_groups=mesh['dp'=2,'wide'=4,'narrow'=4] {'narrow'}, dimensions={2} | all-to-all | bytes 2457600 | tf_op jit(solution)/shard_map/all_to_all | solution.py:104
  1145.6 56.5 %all-gather.23.cloned.1.call-done = bf16[2048,1200]{0,1:T(8,128)(2,1)} async-done(((bf16[512,1200]{0,1:T(8,128)(2,1)}), bf16[2048,1200]{0,1:T(8,128)(2,1)}) %all-gather.23.cloned.1.call-update) | async-done | bytes 4915216 | tf_op jit(solution)/shard_map/all_gather | solution.py:79
  1202.1 6.8 fusion.85
  1209.0 8.2 fusion.88
  1217.2 7.7 convolution_bitcast_fusion
  1224.9 1.9 fusion.87
  1226.8 4.2 fusion.86
  1231.4 4.6 fusion.8
  1237.0 42.9 %all-reduce = (f32[2,1600]{1,0:T(2,128)S(1)}, f32[6400]{0:T(1024)S(1)}) all-reduce(f32[2,1600]{1,0:T(2,128)S(1)} %pad_maximum_fusion.1, f32[6400]{0:T(1024)S(1)} %dynamic_update_slice.3), channel_id=1, replica_groups=mesh['dp'=2,'wide'=4,'narrow'=4] {'dp','wide','narrow'}, use_global_device_ids=true, to_apply=%region_32.33 | all-reduce | flops 9600 | bytes 76800 | tf_op jit(solution)/shard_map/psum | solution.py:233
  1281.3 1.8 multiply_reduce_fusion.2
  1283.1 9.7 all-reduce.2
  1292.8 28.2 %all-reduce.1 = (f32[400]{0:T(512)}, f32[400]{0:T(512)}, f32[400]{0:T(512)}, f32[400]{0:T(512)}, f32[400]{0:T(512)}, /*index=5*/f32[400]{0:T(512)}) all-reduce(f32[400]{0:T(512)S(1)} %get-tuple-element.114, f32[400]{0:T(512)S(1)} %get-tuple-element.119, ...), channel_id=1, replica_groups=mesh['dp'=2,'wide'=4,'narrow'=4] {'dp','narrow'}, use_global_device_ids=true, to_apply=%region_27.28 | all-reduce | flops 2400 | bytes 19200 | tf_op jit(solution)/shard_map/psum | solution.py:245
  1322.2 3.3 copy.154
  1326.4 1.5 copy.176
  1329.1 1.5 copy.177
  (145 shorter events, 27.3 us)
Async XLA Ops:
  7.2 14.0 %copy-start = (f32[400,512]{1,0:T(8,128)S(1)}, f32[400,512]{1,0:T(8,128)}, u32[]{:S(2)}) copy-start(f32[400,512]{1,0:T(8,128)} %param.15) | copy-start | bytes 2457604
  7.2 14.0 %copy-start.20 = (f32[400]{0:T(512)S(1)}, f32[400]{0:T(512)}, u32[]{:S(2)}) copy-start(f32[400]{0:T(512)} %param.18) | copy-start | bytes 4804
  7.2 14.0 %copy-start.24 = (f32[400]{0:T(512)S(1)}, f32[400]{0:T(512)}, u32[]{:S(2)}) copy-start(f32[400]{0:T(512)} %param.19) | copy-start | bytes 4804
  7.2 52.6 %all-gather.9.cloned.1.call-start = ((), (), s32[]{:S(2)}) async-start(), calls=%async_computation.12 | async-start | bytes 2048000 | tf_op jit(solution)/shard_map/all_gather | solution.py:49
  22.2 141.4 %reduce-scatter.9.cloned.1.call-start = ((), (), s32[]{:S(2)}) async-start(), calls=%async_computation.13 | async-start | bytes 12288000 | tf_op jit(solution)/shard_map/reduce_scatter | solution.py:65
  24.9 41.5 %copy-start.17 = (bf16[400,3,400]{0,2,1:T(8,128)(2,1)}, bf16[400,3,400]{0,2,1:T(8,128)(2,1)S(1)}, u32[]{:S(2)}) copy-start(bf16[400,3,400]{0,2,1:T(8,128)(2,1)S(1)} %copy.134) | copy-start | bytes 2880004
  66.5 0.7 copy-start.23
  168.5 4.9 copy-start.27
  168.5 52.7 %all-to-all-start = ((bf16[512,3,400]{2,1,0:T(4,128)(2,1)}), bf16[512,3,400]{2,1,0:T(4,128)(2,1)S(1)}, u32[]{:S(2)}, u32[]{:S(2)}) async-start(bf16[512,3,400]{2,1,0:T(4,128)(2,1)} %copy.135), calls=%async_computation.1 | async-start | bytes 4194304 | tf_op jit(solution)/shard_map/all_to_all | solution.py:100
  173.2 115.3 %all-gather.11.cloned.1.call-start = ((), (), s32[]{:S(2)}) async-start(), calls=%async_computation.14 | async-start | bytes 2048000 | tf_op jit(solution)/shard_map/all_gather | solution.py:71
  225.1 0.8 copy-start.7
  225.1 1.2 copy-start.9
  225.1 1.9 copy-start.12
  226.3 1.2 copy-start.15
  257.9 30.6 %copy-start.2 = (f32[400,400]{1,0:T(8,128)S(1)}, f32[400,400]{1,0:T(8,128)}, u32[]{:S(2)}) copy-start(f32[400,400]{1,0:T(8,128)} %param.22) | copy-start | bytes 1920004
  258.9 96.3 %reduce-scatter.11.cloned.1.call-start = ((), (), s32[]{:S(2)}) async-start(), calls=%async_computation.15 | async-start | bytes 4096000 | tf_op jit(solution)/shard_map/reduce_scatter | solution.py:53
  292.6 1.1 copy-start.4
  292.6 62.6 %copy-start.28 = (f32[400]{0:T(512)S(1)}, f32[400]{0:T(512)}, u32[]{:S(2)}) copy-start(f32[400]{0:T(512)} %param.23) | copy-start | bytes 4804
  292.7 102.7 %all-gather.17.cloned.1.call-start = ((), (), s32[]{:S(2)}) async-start(), calls=%async_computation.20 | async-start | bytes 2048000 | tf_op jit(solution)/shard_map/all_gather | solution.py:49
  294.6 71.9 %copy-start.19 = (f32[400]{0:T(512)S(1)}, f32[400]{0:T(512)}, u32[]{:S(2)}) copy-start(f32[400]{0:T(512)} %param.24) | copy-start | bytes 4804
  294.6 71.9 %copy-start.25 = (f32[400]{0:T(512)S(1)}, f32[400]{0:T(512)}, u32[]{:S(2)}) copy-start(f32[400]{0:T(512)} %param.25) | copy-start | bytes 4804
  294.6 139.8 %all-gather.13.cloned.1.call-start = ((), (), s32[]{:S(2)}) async-start(), calls=%async_computation.16 | async-start | bytes 2048000 | tf_op jit(solution)/shard_map/all_gather | solution.py:49
  367.4 193.8 %reduce-scatter.17.cloned.1.call-start = ((), (), s32[]{:S(2)}) async-start(), calls=%async_computation.21 | async-start | bytes 16384000 | tf_op jit(solution)/shard_map/reduce_scatter | solution.py:65
  406.0 283.3 %reduce-scatter.13.cloned.1.call-start = ((), (), s32[]{:S(2)}) async-start(), calls=%async_computation.17 | async-start | bytes 16384000 | tf_op jit(solution)/shard_map/reduce_scatter | solution.py:65
  445.6 243.7 %copy-start.21 = (f32[1600]{0:T(1024)S(1)}, f32[1600]{0:T(1024)}, u32[]{:S(2)}) copy-start(f32[1600]{0:T(1024)} %param.27) | copy-start | bytes 19204
  445.6 321.8 %all-gather.19.cloned.1.call-start = ((), (), s32[]{:S(2)}) async-start(), calls=%async_computation.22 | async-start | bytes 8192000 | tf_op jit(solution)/shard_map/all_gather | solution.py:79
  695.2 146.6 %all-gather.15.cloned.1.call-start = ((), (), s32[]{:S(2)}) async-start(), calls=%async_computation.18 | async-start | bytes 8192000 | tf_op jit(solution)/shard_map/all_gather | solution.py:71
  695.8 210.8 %reduce-scatter.19.cloned.1.call-start = ((), (), s32[]{:S(2)}) async-start(), calls=%async_computation.23 | async-start | bytes 4096000 | tf_op jit(solution)/shard_map/reduce_scatter | solution.py:53
  775.9 195.3 %reduce-scatter.15.cloned.1.call-start = ((), (), s32[]{:S(2)}) async-start(), calls=%async_computation.19 | async-start | bytes 4096000 | tf_op jit(solution)/shard_map/reduce_scatter | solution.py:53
  850.3 120.9 %copy-start.26 = (f32[400]{0:T(512)S(1)}, f32[400]{0:T(512)}, u32[]{:S(2)}) copy-start(f32[400]{0:T(512)} %param.29) | copy-start | bytes 4804
  850.3 163.4 %all-gather.21.cloned.1.call-start = ((), (), s32[]{:S(2)}) async-start(), calls=%async_computation.24 | async-start | bytes 2048000 | tf_op jit(solution)/shard_map/all_gather | solution.py:49
  975.5 86.4 %reduce-scatter.21.cloned.1.call-start = ((), (), s32[]{:S(2)}) async-start(), calls=%async_computation.25 | async-start | bytes 4096000 | tf_op jit(solution)/shard_map/reduce_scatter | solution.py:65
  1063.1 9.2 copy-start.8
  1063.1 9.2 copy-start.10
  1067.7 16.5 %all-to-all-start.2 = ((bf16[4,2,25600]{2,1,0:T(2,128)(2,1)}), bf16[4,2,25600]{2,1,0:T(2,128)(2,1)S(1)}, u32[]{:S(2)}, u32[]{:S(2)}) async-start(bf16[4,2,25600]{2,1,0:T(2,128)(2,1)} %reshape.92), calls=%async_computation.9 | async-start | bytes 819200 | tf_op jit(solution)/shard_map/all_to_all | solution.py:100
  1072.4 129.8 %all-gather.23.cloned.1.call-start = ((), (), s32[]{:S(2)}) async-start(), calls=%async_computation.26 | async-start | bytes 6144000 | tf_op jit(solution)/shard_map/all_gather | solution.py:79
  1085.5 1.7 copy-start.13
  1086.3 2.4 copy-start.11
  1086.4 0.8 copy-start.14
  1145.4 135.8 %reduce-scatter.23.cloned.1.call-start = ((), (), s32[]{:S(2)}) async-start(), calls=%async_computation.27 | async-start | bytes 4096000 | tf_op jit(solution)/shard_map/reduce_scatter | solution.py:53
  1208.9 113.3 %all-reduce.9.cloned.1.call-start = ((), (), s32[]{:S(2)}) async-start(), calls=%async_computation.28 | async-start | bytes 17203200 | tf_op jit(solution)/shard_map/psum | solution.py:250
  1209.0 8.2 copy-start.30
  1209.0 17.8 %slice-start = ((s8[4915200]{0:T(1024)(128)(4,1)}), s8[720896]{0:T(1024)(128)(4,1)S(1)}, s32[]{:S(2)}) async-start(s8[4915200]{0:T(1024)(128)(4,1)} %bitcast.192), calls=%async_computation.29 | async-start | bytes 1441792
  1217.2 7.7 copy-start.1
  1217.2 7.7 copy-start.16
  1217.2 9.6 slice-start.1
  1224.9 1.9 copy-start.29
  1236.3 56.5 %copy-start.22 = (f32[400]{0:T(512)S(1)}, f32[400]{0:T(512)}, u32[]{:S(2)}) copy-start(f32[400]{0:T(512)} %get-tuple-element.144) | copy-start | bytes 4804
  1281.2 39.8 %copy-start.3 = (f32[512,400]{0,1:T(8,128)S(1)}, f32[512,400]{0,1:T(8,128)}, u32[]{:S(2)}) copy-start(f32[512,400]{0,1:T(8,128)} %reduce-scatter.23.cloned.1.call-done) | copy-start | bytes 2457604
  1322.2 3.3 copy-start.18
  1322.2 4.2 copy-start.6
  1326.4 2.7 copy-start.5
Sparse Core Ops, SparseCore 0:
  22.3 37.4 all-gather.8
  66.6 96.9 reduce-scatter.8
  259.1 29.3 all-gather.10
  292.8 62.4 reduce-scatter.10
  357.2 38.0 all-gather.16
  397.3 36.9 all-gather.12
  437.5 123.7 reduce-scatter.16
  564.4 124.8 reduce-scatter.12
  695.3 72.0 all-gather.18
  769.7 72.0 all-gather.14
  844.1 62.4 reduce-scatter.18
  908.7 62.4 reduce-scatter.14
  975.6 38.0 all-gather.20
  1018.0 43.8 reduce-scatter.20
  1145.5 56.5 all-gather.22
  1209.0 63.3 reduce-scatter.22
  1276.3 38.5 all-reduce.8
where the time goes:
time: 1340 us
  waiting for transfers between devices  964 us (72%)
  blocking collectives  166 us (12%)
  matrix products  98.5 us (7%)
  other arithmetic  45.2 us (3%)
  local copies, waits for them, and re-layouts  37.6 us (3%)
  between operations  14.7 us (1%)
    reduce_scatter x4, waiting for transfers between devices, sum_wide(): lax.psum_scatter(partial_rows(), 'wide', scatter_dimension=0, tiled=True)  384 us
    reduce_scatter x4, waiting for transfers between devices, sum_narrow(): lax.psum_scatter(partial_value, 'narrow', scatter_dimension=0, tiled=True)  170 us
    all_gather x4, waiting for transfers between devices, gather_narrow(): return lax.all_gather(values, 'narrow', axis=0, tiled=True)  129 us
    all_gather x2, waiting for transfers between devices, fold_wide(): block_rows = lax.all_gather(grad_rows, 'wide', axis=0, tiled=True)  128 us
    all_gather x2, waiting for transfers between devices, project_wide(): lax.all_gather(activations, 'wide', axis=0, tiled=True)  94.9 us
    all_to_all x2, waiting for transfers between devices, to_heads(): lax.all_to_all(values, 'narrow', split_axis=0, concat_axis=2, tiled=True)  57.5 us
    all_to_all x2, blocking collectives, from_heads(): lax.all_to_all(values, 'narrow', split_axis=2, concat_axis=0, tiled=True)  54.3 us
    psum x1, blocking collectives, local(): lax.psum((bias_qv_full, fc_full), ('dp', 'wide', 'narrow'))  42.9 us
  transfers between devices with their start and end apart: 19, of which 17 were waited for; matrix products, arithmetic and copies ran while one was open for 6% of the time, Pallas kernels for 0%

commit v1 on v0

--- a/solution.py
+++ b/solution.py
@@ -8,6 +8,28 @@
 HEAD = 64
 EPS = 1e-05
 GELU_C = math.sqrt(2.0 / math.pi)
+
+
+def laid_out(pieces, dim):
+    lengths = list(pieces.shape[1:])
+    lengths[dim] *= pieces.shape[0]
+    return jnp.moveaxis(pieces, 0, dim).reshape(lengths)
+
+
+def collected_by_bits(array, axis):
+    size = lax.axis_size(axis)
+    blocks = array[None]
+    for level in range(size.bit_length() - 1):
+        distance = 1 << level
+        other = lax.ppermute(blocks, axis, [(i, i ^ distance) for i in range(size)])
+        both = jnp.stack([blocks, other])
+        upper = lax.axis_index(axis) >> level & 1
+        blocks = jnp.where(upper == 0, both, both[::-1]).reshape(-1, *array.shape)
+    return blocks
+
+
+def doubled_up(x, axis, dim):
+    return laid_out(collected_by_bits(x, axis), dim)
 
 
 def gelu_value(pre_act):
@@ -67,11 +89,7 @@
 
 def project_wide(activations, weight_bf):
     return sum_narrow(
-        jnp.dot(
-            lax.all_gather(activations, "wide", axis=0, tiled=True),
-            weight_bf,
-            preferred_element_type=jnp.float32,
-        )
+        jnp.dot(doubled_up(activations, "wide", 0), weight_bf, preferred_element_type=jnp.float32)
     )
 
 

time: 1340 us -> 1420 us (1.060)
  waiting for transfers between devices: 964 us -> 1010 us
  local copies, waits for them, and re-layouts: 37.6 us -> 52.7 us
    ppermute x0 -> x4, waiting for transfers between devices: none -> 96.4 us  [collected_by_bits(): other = lax.ppermute(blocks, axis, [(i, i ^ distance) for i in range(size)])]
    reduce_scatter x4, waiting for transfers between devices: 170 us -> 115 us  [sum_narrow(): lax.psum_scatter(partial_value, 'narrow', scatter_dimension=0, tiled=True)]
    all_gather x2, waiting for transfers between devices: 128 us -> 144 us  [fold_wide(): block_rows = lax.all_gather(grad_rows, 'wide', axis=0, tiled=True)]
  transfers between devices with their start and end apart: 19 -> 23, of which waited for: 17 -> 21; matrix products, arithmetic and copies ran while one was open for 6% -> 8% of each run, Pallas kernels for 0% -> 0%
where the time goes in v1:
time: 1420 us
  waiting for transfers between devices  1010 us (71%)
  blocking collectives  165 us (12%)
  matrix products  105 us (7%)
  other arithmetic  53.6 us (4%)
  local copies, waits for them, and re-layouts  52.7 us (4%)
  starting transfers between devices  17.3 us (1%)
  between operations  14.8 us (1%)
    reduce_scatter x4, waiting for transfers between devices, sum_wide(): lax.psum_scatter(partial_rows(), 'wide', scatter_dimension=0, tiled=True)  384 us
    all_gather x2, waiting for transfers between devices, fold_wide(): block_rows = lax.all_gather(grad_rows, 'wide', axis=0, tiled=True)  144 us
    all_gather x4, waiting for transfers between devices, gather_narrow(): return lax.all_gather(values, 'narrow', axis=0, tiled=True)  129 us
    reduce_scatter x4, waiting for transfers between devices, sum_narrow(): lax.psum_scatter(partial_value, 'narrow', scatter_dimension=0, tiled=True)  115 us
    ppermute x4, waiting for transfers between devices, collected_by_bits(): other = lax.ppermute(blocks, axis, [(i, i ^ distance) for i in range(size)])  96.4 us
    all_gather x2, waiting for transfers between devices, weight_grad_block(): lax.all_gather(activations, 'wide', axis=0, tiled=True)  82.5 us
    all_to_all x2, waiting for transfers between devices, to_heads(): lax.all_to_all(values, 'narrow', split_axis=0, concat_axis=2, tiled=True)  57.3 us
    all_to_all x2, blocking collectives, from_heads(): lax.all_to_all(values, 'narrow', split_axis=2, concat_axis=0, tiled=True)  54.5 us
  transfers between devices with their start and end apart: 23, of which 21 were waited for; matrix products, arithmetic and copies ran while one was open for 8% of the time, Pallas kernels for 0%

profile of v1, /device:TPU:0, one launch (start us, length us, event | category | flops | bytes accessed | tf_op | source)
XLA Modules:
  0.0 1419.7 jit_solution(283676790046007548)
XLA Ops:
  9.8 11.4 all-reduce.5
  22.2 1.9 convert_element_type.65
  25.0 34.8 %all-gather.9.cloned.1.call-done = bf16[2048,400]{0,1:T(8,128)(2,1)} async-done(((bf16[512,400]{0,1:T(8,128)(2,1)}), bf16[2048,400]{0,1:T(8,128)(2,1)}) %all-gather.9.cloned.1.call-update) | async-done | bytes 1638416 | tf_op jit(solution)/shard_map/all_gather | solution.py:71
  59.8 6.7 fusion.93
  67.2 96.4 %reduce-scatter.9.cloned.1.call-done = f32[512,1200]{0,1:T(8,128)} async-done(((f32[2048,1200]{0,1:T(8,128)}), f32[512,1200]{0,1:T(8,128)}) %reduce-scatter.9.cloned.1.call-update) | async-done | bytes 2457616 | tf_op jit(solution)/shard_map/reduce_scatter | solution.py:87
  163.6 1.9 add_convert_fusion
  165.5 3.0 copy.156
  168.5 4.7 all-to-all-start
  173.5 47.8 %all-to-all-done = bf16[512,3,400]{2,1,0:T(4,128)(2,1)S(1)} async-done(((bf16[512,3,400]{2,1,0:T(4,128)(2,1)}), bf16[512,3,400]{2,1,0:T(4,128)(2,1)S(1)}, u32[]{:S(2)}, u32[]{:S(2)}) %all-to-all-start) | async-done | bytes 1228832 | tf_op jit(solution)/shard_map/all_to_all | solution.py:118
  221.2 2.5 copy.157
  227.4 6.3 copy.193
  234.3 9.1 reduce.2
  243.5 14.2 all_to_all.63
  260.2 8.5 collective-permute-done
  271.3 16.7 %collective-permute-done.1 = bf16[2,512,400]{1,2,0:T(8,128)(2,1)S(1)} collective-permute-done((bf16[2,512,400]{1,2,0:T(8,128)(2,1)}, bf16[2,512,400]{1,2,0:T(8,128)(2,1)S(1)}, u32[]{:S(2)}, u32[]{:S(2)}) %collective-permute-start.1) | collective-permute-done | bytes 819232 | tf_op jit(solution)/shard_map/ppermute | solution.py:24
  290.2 2.1 reshape_reshape.9
  292.3 4.1 fusion.59
  298.5 59.8 %reduce-scatter.11.cloned.1.call-done = f32[512,400]{0,1:T(8,128)} async-done(((f32[2048,400]{0,1:T(8,128)}), f32[512,400]{0,1:T(8,128)}) %reduce-scatter.11.cloned.1.call-update) | async-done | bytes 819216 | tf_op jit(solution)/shard_map/reduce_scatter | solution.py:75
  359.6 9.9 all-reduce.4
  370.5 27.9 %all-gather.13.cloned.1.call-done = bf16[2048,400]{0,1:T(8,128)(2,1)} async-done(((bf16[512,400]{0,1:T(8,128)(2,1)}), bf16[2048,400]{0,1:T(8,128)(2,1)}) %all-gather.13.cloned.1.call-update) | async-done | bytes 1638416 | tf_op jit(solution)/shard_map/all_gather | solution.py:71
  398.4 10.6 fusion.36
  409.3 28.0 %all-gather.11.cloned.1.call-done = bf16[2048,400]{0,1:T(8,128)(2,1)} async-done(((bf16[512,400]{0,1:T(8,128)(2,1)}), bf16[2048,400]{0,1:T(8,128)(2,1)}) %all-gather.11.cloned.1.call-update) | async-done | bytes 1638416 | tf_op jit(solution)/shard_map/all_gather | solution.py:71
  437.4 11.3 fusion.42
  448.7 115.4 %reduce-scatter.17.cloned.1.call-done = f32[512,1600]{0,1:T(8,128)} async-done(((f32[2048,1600]{0,1:T(8,128)}), f32[512,1600]{0,1:T(8,128)}) %reduce-scatter.17.cloned.1.call-update) | async-done | bytes 3276816 | tf_op jit(solution)/shard_map/reduce_scatter | solution.py:87
  564.1 128.0 %reduce-scatter.13.cloned.1.call-done = f32[512,1600]{0,1:T(8,128)} async-done(((f32[2048,1600]{0,1:T(8,128)}), f32[512,1600]{0,1:T(8,128)}) %reduce-scatter.13.cloned.1.call-update) | async-done | bytes 3276816 | tf_op jit(solution)/shard_map/reduce_scatter | solution.py:87
  692.2 5.7 fusion.79
  699.5 88.8 %all-gather.15.cloned.1.call-done = bf16[2048,1600]{0,1:T(8,128)(2,1)} async-done(((bf16[512,1600]{0,1:T(8,128)(2,1)}), bf16[2048,1600]{0,1:T(8,128)(2,1)}) %all-gather.15.cloned.1.call-update) | async-done | bytes 6553616 | tf_op jit(solution)/shard_map/all_gather | solution.py:97
  788.3 8.5 fusion.40
  797.4 1.7 pad_maximum_fusion.1
  801.5 71.2 %collective-permute-done.3 = bf16[2,512,1600]{1,2,0:T(8,128)(2,1)S(1)} collective-permute-done((bf16[2,512,1600]{1,2,0:T(8,128)(2,1)S(1)}, bf16[2,512,1600]{1,2,0:T(8,128)(2,1)S(1)}, u32[]{:S(2)}, u32[]{:S(2)}) %collective-permute-start.3) | collective-permute-done | bytes 3276832 | tf_op jit(solution)/shard_map/ppermute | solution.py:24
  873.4 4.2 reverse_select_fusion
  877.5 9.8 copy.163
  887.3 8.5 fusion.38
  897.6 9.1 all-reduce.3
  906.7 51.9 %reduce-scatter.15.cloned.1.call-done = f32[512,400]{0,1:T(8,128)} async-done(((f32[2048,400]{0,1:T(8,128)}), f32[512,400]{0,1:T(8,128)}) %reduce-scatter.15.cloned.1.call-update) | async-done | bytes 819216 | tf_op jit(solution)/shard_map/reduce_scatter | solution.py:75
  958.5 3.2 fusion.81
  962.7 38.2 %all-gather.17.cloned.1.call-done = bf16[2048,400]{0,1:T(8,128)(2,1)} async-done(((bf16[512,400]{0,1:T(8,128)(2,1)}), bf16[2048,400]{0,1:T(8,128)(2,1)}) %all-gather.17.cloned.1.call-update) | async-done | bytes 1638416 | tf_op jit(solution)/shard_map/all_gather | solution.py:71
  1000.8 4.2 fusion.57
  1005.0 44.0 %reduce-scatter.21.cloned.1.call-done = f32[512,400]{0,1:T(8,128)} async-done(((f32[2048,400]{0,1:T(8,128)}), f32[512,400]{0,1:T(8,128)}) %reduce-scatter.21.cloned.1.call-update) | async-done | bytes 819216 | tf_op jit(solution)/shard_map/reduce_scatter | solution.py:87
  1050.2 1.7 reduce.3
  1053.1 1.7 reshape.102
  1054.9 4.6 all-to-all-start.2
  1059.7 2.1 fusion.13
  1061.8 9.5 all-to-all-done.2
  1075.9 3.6 fusion.24
  1079.5 3.9 fusion.21
  1083.4 4.0 fusion.46
  1087.4 3.4 fusion.11
  1090.7 40.4 %all_to_all.64 = bf16[128,3,1600]{0,1,2:T(4,128)(2,1)S(1)} all-to-all(bf16[128,3,1600]{0,1,2:T(4,128)(2,1)S(1)} %fusion.11), channel_id=1, replica_groups=mesh['dp'=2,'wide'=4,'narrow'=4] {'narrow'}, dimensions={2} | all-to-all | bytes 2457600 | tf_op jit(solution)/shard_map/all_to_all | solution.py:122
  1134.9 54.9 %all-gather.19.cloned.1.call-done = bf16[2048,1200]{0,1:T(8,128)(2,1)} async-done(((bf16[512,1200]{0,1:T(8,128)(2,1)}), bf16[2048,1200]{0,1:T(8,128)(2,1)}) %all-gather.19.cloned.1.call-update) | async-done | bytes 4915216 | tf_op jit(solution)/shard_map/all_gather | solution.py:97
  1189.8 6.8 fusion.89
  1196.8 9.2 fusion.92
  1206.0 57.5 %all-gather.23.cloned.1.call-done = bf16[2048,1600]{0,1:T(8,128)(2,1)} async-done(((bf16[512,1600]{0,1:T(8,128)(2,1)}), bf16[2048,1600]{0,1:T(8,128)(2,1)}) %all-gather.23.cloned.1.call-update) | async-done | bytes 6553616 | tf_op jit(solution)/shard_map/all_gather | solution.py:110
  1263.6 8.0 convolution_bitcast_fusion
  1271.5 25.0 %all-gather.21.cloned.1.call-done = bf16[2048,400]{0,1:T(8,128)(2,1)} async-done(((bf16[512,400]{0,1:T(8,128)(2,1)}), bf16[2048,400]{0,1:T(8,128)(2,1)}) %all-gather.21.cloned.1.call-update) | async-done | bytes 1638416 | tf_op jit(solution)/shard_map/all_gather | solution.py:110
  1296.5 4.0 fusion.91
  1300.5 6.6 fusion.90
  1308.2 4.6 fusion.10
  1313.8 43.8 %all-reduce = (f32[2,1600]{1,0:T(2,128)S(1)}, f32[6400]{0:T(1024)S(1)}) all-reduce(f32[2,1600]{1,0:T(2,128)S(1)} %pad_maximum_fusion.5, f32[6400]{0:T(1024)S(1)} %dynamic_update_slice.3), channel_id=1, replica_groups=mesh['dp'=2,'wide'=4,'narrow'=4] {'dp','wide','narrow'}, use_global_device_ids=true, to_apply=%region_32.33 | all-reduce | flops 9600 | bytes 76800 | tf_op jit(solution)/shard_map/psum | solution.py:251
  1358.9 3.2 reduce-scatter.23.cloned.1.call-done
  1363.7 9.8 all-reduce.2
  1373.5 27.0 %all-reduce.1 = (f32[400]{0:T(512)}, f32[400]{0:T(512)}, f32[400]{0:T(512)}, f32[400]{0:T(512)}, f32[400]{0:T(512)}, /*index=5*/f32[400]{0:T(512)}) all-reduce(f32[400]{0:T(512)S(1)} %get-tuple-element.114, f32[400]{0:T(512)S(1)} %get-tuple-element.119, ...), channel_id=1, replica_groups=mesh['dp'=2,'wide'=4,'narrow'=4] {'dp','narrow'}, use_global_device_ids=true, to_apply=%region_27.28 | all-reduce | flops 2400 | bytes 19200 | tf_op jit(solution)/shard_map/psum | solution.py:263
  1401.7 2.8 all-reduce.9.cloned.1.call-done
  1404.5 3.3 copy.179
  (169 shorter events, 51.6 us)
Async XLA Ops:
  7.2 14.0 copy-start
  7.2 14.0 copy-start.25
  7.2 14.0 copy-start.29
  7.2 52.6 %all-gather.9.cloned.1.call-start = ((), (), s32[]{:S(2)}) async-start(), calls=%async_computation.12 | async-start | bytes 2048000 | tf_op jit(solution)/shard_map/all_gather | solution.py:71
  22.2 141.4 %reduce-scatter.9.cloned.1.call-start = ((), (), s32[]{:S(2)}) async-start(), calls=%async_computation.13 | async-start | bytes 12288000 | tf_op jit(solution)/shard_map/reduce_scatter | solution.py:87
  24.9 41.5 %copy-start.22 = (bf16[400,3,400]{0,2,1:T(8,128)(2,1)}, bf16[400,3,400]{0,2,1:T(8,128)(2,1)S(1)}, u32[]{:S(2)}) copy-start(bf16[400,3,400]{0,2,1:T(8,128)(2,1)S(1)} %copy.155) | copy-start | bytes 2880004
  66.5 0.7 copy-start.28
  168.5 4.9 copy-start.32
  168.5 52.7 %all-to-all-start = ((bf16[512,3,400]{2,1,0:T(4,128)(2,1)}), bf16[512,3,400]{2,1,0:T(4,128)(2,1)S(1)}, u32[]{:S(2)}, u32[]{:S(2)}) async-start(bf16[512,3,400]{2,1,0:T(4,128)(2,1)} %copy.156), calls=%async_computation.1 | async-start | bytes 4194304 | tf_op jit(solution)/shard_map/all_to_all | solution.py:118
  173.2 185.1 %reduce-scatter.11.cloned.1.call-start = ((), (), s32[]{:S(2)}) async-start(), calls=%async_computation.14 | async-start | bytes 4096000 | tf_op jit(solution)/shard_map/reduce_scatter | solution.py:75
  225.1 0.7 copy-start.13
  225.1 1.2 copy-start.15
  225.1 1.9 copy-start.18
  226.2 1.2 copy-start.21
  258.3 10.4 copy-start.2
  258.5 10.2 collective-permute-start
  269.8 18.2 %collective-permute-start.1 = (bf16[2,512,400]{1,2,0:T(8,128)(2,1)}, bf16[2,512,400]{1,2,0:T(8,128)(2,1)S(1)}, u32[]{:S(2)}, u32[]{:S(2)}) collective-permute-start(bf16[2,512,400]{1,2,0:T(8,128)(2,1)} %get-tuple-element.159), channel_id=1, source_target_pairs={{0,8},{4,12},{8,0},{12,4},{1,9},{5,13},{9,1},{13,5},{2,10},{6,14},... | collective-permute-start | bytes 2457608 | tf_op jit(solution)/shard_map/ppermute | solution.py:24
  290.2 2.1 copy-start.4
  296.4 1.1 copy-start.7
  296.5 61.8 %copy-start.33 = (f32[400]{0:T(512)S(1)}, f32[400]{0:T(512)}, u32[]{:S(2)}) copy-start(f32[400]{0:T(512)} %param.23) | copy-start | bytes 4804
  296.5 101.9 %all-gather.13.cloned.1.call-start = ((), (), s32[]{:S(2)}) async-start(), calls=%async_computation.18 | async-start | bytes 2048000 | tf_op jit(solution)/shard_map/all_gather | solution.py:71
  298.4 71.1 %copy-start.24 = (f32[400]{0:T(512)S(1)}, f32[400]{0:T(512)}, u32[]{:S(2)}) copy-start(f32[400]{0:T(512)} %param.24) | copy-start | bytes 4804
  298.4 71.1 %copy-start.30 = (f32[400]{0:T(512)S(1)}, f32[400]{0:T(512)}, u32[]{:S(2)}) copy-start(f32[400]{0:T(512)} %param.25) | copy-start | bytes 4804
  298.4 139.0 %all-gather.11.cloned.1.call-start = ((), (), s32[]{:S(2)}) async-start(), calls=%async_computation.15 | async-start | bytes 2048000 | tf_op jit(solution)/shard_map/all_gather | solution.py:71
  370.5 193.6 %reduce-scatter.17.cloned.1.call-start = ((), (), s32[]{:S(2)}) async-start(), calls=%async_computation.19 | async-start | bytes 16384000 | tf_op jit(solution)/shard_map/reduce_scatter | solution.py:87
  409.0 283.1 %reduce-scatter.13.cloned.1.call-start = ((), (), s32[]{:S(2)}) async-start(), calls=%async_computation.16 | async-start | bytes 16384000 | tf_op jit(solution)/shard_map/reduce_scatter | solution.py:87
  448.6 243.5 %copy-start.26 = (f32[1600]{0:T(1024)S(1)}, f32[1600]{0:T(1024)}, u32[]{:S(2)}) copy-start(f32[1600]{0:T(1024)} %param.27) | copy-start | bytes 19204
  448.7 339.6 %all-gather.15.cloned.1.call-start = ((), (), s32[]{:S(2)}) async-start(), calls=%async_computation.20 | async-start | bytes 8192000 | tf_op jit(solution)/shard_map/all_gather | solution.py:97
  697.9 99.5 %copy-start.1 = (bf16[512,1600]{0,1:T(8,128)(2,1)}, bf16[512,1600]{0,1:T(8,128)(2,1)S(1)}, u32[]{:S(2)}) copy-start(bf16[512,1600]{0,1:T(8,128)(2,1)S(1)} %get-tuple-element.147) | copy-start | bytes 4915204
  697.9 198.1 %reduce-scatter.19.cloned.1.call-start = ((), (), s32[]{:S(2)}) async-start(), calls=%async_computation.21 | async-start | bytes 4096000 | tf_op jit(solution)/shard_map/reduce_scatter | solution.py:75
  698.0 99.4 %collective-permute-start.2 = (bf16[1,512,1600]{1,2,0:T(8,128)(2,1)S(1)}, bf16[1,512,1600]{1,2,0:T(8,128)(2,1)}, u32[]{:S(2)}, u32[]{:S(2)}) collective-permute-start(bf16[1,512,1600]{1,2,0:T(8,128)(2,1)S(1)} %bitcast.156), channel_id=1, source_target_pairs={{0,4},{4,0},{8,12},{12,8},{1,5},{5,1},{9,13},{13,9},{2,6},{6,2},{1... | collective-permute-start | bytes 4915208 | tf_op jit(solution)/shard_map/ppermute | solution.py:24
  796.9 161.7 %reduce-scatter.15.cloned.1.call-start = ((), (), s32[]{:S(2)}) async-start(), calls=%async_computation.17 | async-start | bytes 4096000 | tf_op jit(solution)/shard_map/reduce_scatter | solution.py:75
  800.0 72.8 %collective-permute-start.3 = (bf16[2,512,1600]{1,2,0:T(8,128)(2,1)S(1)}, bf16[2,512,1600]{1,2,0:T(8,128)(2,1)S(1)}, u32[]{:S(2)}, u32[]{:S(2)}) collective-permute-start(bf16[2,512,1600]{1,2,0:T(8,128)(2,1)S(1)} %get-tuple-element.149), channel_id=1, source_target_pairs={{0,8},{4,12},{8,0},{12,4},{1,9},{5,13},{9,1},{13,5},{2,10},{6,14},... | collective-permute-start | bytes 9830408 | tf_op jit(solution)/shard_map/ppermute | solution.py:24
  895.9 62.6 %copy-start.8 = (f32[400,512]{1,0:T(8,128)S(1)}, f32[400,512]{1,0:T(8,128)}, u32[]{:S(2)}) copy-start(f32[400,512]{1,0:T(8,128)} %param.16) | copy-start | bytes 2457604
  895.9 62.6 %copy-start.31 = (f32[400]{0:T(512)S(1)}, f32[400]{0:T(512)}, u32[]{:S(2)}) copy-start(f32[400]{0:T(512)} %param.29) | copy-start | bytes 4804
  895.9 104.9 %all-gather.17.cloned.1.call-start = ((), (), s32[]{:S(2)}) async-start(), calls=%async_computation.22 | async-start | bytes 2048000 | tf_op jit(solution)/shard_map/all_gather | solution.py:71
  961.8 39.1 %copy-start.5 = (f32[400,400]{1,0:T(8,128)S(1)}, f32[400,400]{1,0:T(8,128)}, u32[]{:S(2)}) copy-start(f32[400,400]{1,0:T(8,128)} %param.22) | copy-start | bytes 1920004
  962.6 86.4 %reduce-scatter.21.cloned.1.call-start = ((), (), s32[]{:S(2)}) async-start(), calls=%async_computation.23 | async-start | bytes 4096000 | tf_op jit(solution)/shard_map/reduce_scatter | solution.py:87
  1050.2 9.4 copy-start.14
  1050.2 9.4 copy-start.16
  1054.9 16.5 %all-to-all-start.2 = ((bf16[4,2,25600]{2,1,0:T(2,128)(2,1)}), bf16[4,2,25600]{2,1,0:T(2,128)(2,1)S(1)}, u32[]{:S(2)}, u32[]{:S(2)}) async-start(bf16[4,2,25600]{2,1,0:T(2,128)(2,1)} %reshape.102), calls=%async_computation.9 | async-start | bytes 819200 | tf_op jit(solution)/shard_map/all_to_all | solution.py:118
  1059.5 130.3 %all-gather.19.cloned.1.call-start = ((), (), s32[]{:S(2)}) async-start(), calls=%async_computation.24 | async-start | bytes 6144000 | tf_op jit(solution)/shard_map/all_gather | solution.py:97
  1072.6 1.7 copy-start.19
  1073.5 2.4 copy-start.17
  1073.5 0.8 copy-start.20
  1083.4 4.0 copy-start.9
  1133.0 1.0 copy-start.3
  1133.0 130.5 %all-gather.23.cloned.1.call-start = ((), (), s32[]{:S(2)}) async-start(), calls=%async_computation.27 | async-start | bytes 8192000 | tf_op jit(solution)/shard_map/all_gather | solution.py:110
  1133.6 162.9 %all-gather.21.cloned.1.call-start = ((), (), s32[]{:S(2)}) async-start(), calls=%async_computation.26 | async-start | bytes 2048000 | tf_op jit(solution)/shard_map/all_gather | solution.py:110
  1134.9 227.3 %reduce-scatter.23.cloned.1.call-start = ((), (), s32[]{:S(2)}) async-start(), calls=%async_computation.25 | async-start | bytes 4096000 | tf_op jit(solution)/shard_map/reduce_scatter | solution.py:75
  1196.6 207.9 %all-reduce.9.cloned.1.call-start = ((), (), s32[]{:S(2)}) async-start(), calls=%async_computation.28 | async-start | bytes 17203200 | tf_op jit(solution)/shard_map/psum | solution.py:268
  1296.5 4.0 copy-start.34
  1307.1 1.1 copy-start.10
  1313.1 60.4 %copy-start.27 = (f32[400]{0:T(512)S(1)}, f32[400]{0:T(512)}, u32[]{:S(2)}) copy-start(f32[400]{0:T(512)} %get-tuple-element.144) | copy-start | bytes 4804
  1362.1 38.4 %copy-start.6 = (f32[512,400]{0,1:T(8,128)S(1)}, f32[512,400]{0,1:T(8,128)}, u32[]{:S(2)}) copy-start(f32[512,400]{0,1:T(8,128)} %reduce-scatter.23.cloned.1.call-done) | copy-start | bytes 2457604
  1404.5 3.3 copy-start.23
  1404.5 4.2 copy-start.12
  1408.7 2.7 copy-start.11
Sparse Core Ops, SparseCore 0:
  22.3 37.4 all-gather.8
  66.6 96.9 reduce-scatter.8
  296.6 61.6 reduce-scatter.10
  360.3 38.0 all-gather.12
  400.4 36.9 all-gather.10
  440.4 123.7 reduce-scatter.16
  567.3 124.8 reduce-scatter.12
  698.0 90.2 all-gather.14
  797.0 62.4 reduce-scatter.18
  896.0 62.4 reduce-scatter.14
  962.7 38.0 all-gather.16
  1005.2 43.8 reduce-scatter.20
  1133.1 56.5 all-gather.18
  1191.4 72.0 all-gather.22
  1265.2 31.2 all-gather.20
  1298.7 63.4 reduce-scatter.22
  1365.9 38.4 all-reduce.8
